TPU v7x, 32 devices: a whole 2x2x4 slice. The times are simulated.
32 devices in a mesh: gx: 4 (over z), gy: 4 (over x, core), gz: 2 (over y).
Axes of the slice: x: 2, y: 2, z: 4, core: 2. Of those that a mesh axis runs over, the one named last changes fastest.
Arguments:
- inputs: bfloat16 [112, 112, 14, 96], P('gx', 'gy', 'gz'), may hold values from -6 to 6
- d_out: bfloat16 [112, 112, 14, 96], P('gx', 'gy', 'gz'), may hold values from -6 to 6
- layer_norm_gain: float32 [96], replicated, may hold values from 0.1 to 1.9
- layer_norm_bias: float32 [96], replicated, may hold values from -3 to 3
- w_qkv: bfloat16 [96, 288], replicated, may hold values from -0.625 to 0.625
- b_qkv: float32 [288], replicated, may hold values from -3 to 3
- w_proj: bfloat16 [96, 96], replicated, may hold values from -0.625 to 0.625
- rel_bias: float32 [3, 2197], replicated, may hold values from -4 to 240
Outputs:
- d_x: bfloat16 [112, 112, 14, 96], P('gx', 'gy', 'gz')
- g_qkv: float32 [96, 288], replicated
- g_bqkv: float32 [288], replicated
- g_proj: float32 [96, 96], replicated
- g_rel: float32 [3, 2197], replicated
- gain_gradient: float32 [96], replicated
- g_shift: float32 [96], replicated
All inputs are finite; a program needn't handle non-finite values.
Results may differ from a plain program's by a relative error of at most 0.011.
Values may be sent and summed in bfloat16 or wider, within the bound.
No kernel may reach another device: no remote copies, remote signals or barrier semaphores. Data moves between devices by JAX's collectives and lax.ppermute only.
A program may use at most 192 MiB of HBM per device.

v0:
```python
import jax
import jax.numpy as jnp
from jax import lax
from jax.sharding import PartitionSpec as P

WIN = 7
SHIFT = 3


def shifted(block, axis, distance):
    devices = range(lax.axis_size(axis))
    route = [((i - distance) % len(devices), i) for i in devices]
    return lax.ppermute(block, axis, route)


def offset_ones(span):
    first = jnp.arange(span)[:, None, None]
    second = jnp.arange(span)[None, :, None]
    third = jnp.arange(2 * span - 1)[None, None, :]
    return (first - second + span - 1 == third).astype(jnp.float32)


def expand_table(table, span):
    exact = lax.Precision.HIGHEST
    ones = offset_ones(span)
    width = 2 * span - 1
    heads = table.shape[0]
    cube = table.reshape(heads, width, width, width)
    section = jnp.einsum("hxyz,cCz->hxycC", cube, ones, precision=exact)
    section = jnp.einsum("hxycC,bBy->hxbcBC", section, ones, precision=exact)
    section = jnp.einsum("hxbcBC,aAx->habcABC", section, ones, precision=exact)
    return section.reshape(heads, span**3, span**3)


def fold_table(pairs, span):
    exact = lax.Precision.HIGHEST
    ones = offset_ones(span)
    heads = pairs.shape[0]
    grid = pairs.reshape(heads, span, span, span, span, span, span)
    section = jnp.einsum("habcABC,aAx->hxbcBC", grid, ones, precision=exact)
    section = jnp.einsum("hxbcBC,bBy->hxycC", section, ones, precision=exact)
    section = jnp.einsum("hxycC,cCz->hxyz", section, ones, precision=exact)
    return section.reshape(heads, -1)


def region_label(start, cells, count):
    places = start + jnp.arange(cells)
    return jnp.where(places < count - WIN, 0, jnp.where(places < count - SHIFT, 1, 2)).astype(
        jnp.int32
    )


def to_windows(array):
    first, second, third = array.shape[:3]
    rest = array.shape[3:]
    shaped = array.reshape((first // WIN, WIN, second // WIN, WIN, third // WIN, WIN) + rest)
    order = (0, 2, 4, 1, 3, 5) + tuple(range(6, 6 + len(rest)))
    return shaped.transpose(order).reshape((-1, WIN**3) + rest)


def from_windows(array, first, second, third):
    feats = array.shape[-1]
    shaped = array.reshape(first // WIN, second // WIN, third // WIN, WIN, WIN, WIN, feats)
    return shaped.transpose(0, 3, 1, 4, 2, 5, 6).reshape(first, second, third, feats)


def forward_depth(pair):
    arrived = shifted(pair[:, :SHIFT], "gx", -1)
    return jnp.concatenate([pair[:, SHIFT:], arrived], 1)


def forward_height(pair):
    arrived = shifted(pair[:, :, :SHIFT], "gy", -1)
    return jnp.concatenate([pair[:, :, SHIFT:], arrived], 2)


def forward_width(pair):
    arrived = shifted(pair[:, :, :, :SHIFT], "gz", -1)
    return jnp.concatenate([pair[:, :, :, SHIFT:], arrived], 3)


def backward_depth(field):
    edge = field.shape[0] - SHIFT
    arrived = shifted(field[edge:], "gx", 1)
    return jnp.concatenate([arrived, field[:edge]], 0)


def backward_height(field):
    edge = field.shape[1] - SHIFT
    arrived = shifted(field[:, edge:], "gy", 1)
    return jnp.concatenate([arrived, field[:, :edge]], 1)


def backward_width(field):
    edge = field.shape[2] - SHIFT
    arrived = shifted(field[:, :, edge:], "gz", 1)
    return jnp.concatenate([arrived, field[:, :, :edge]], 2)


def window_pass(ln_w, dy_w, lab_w, w_qkv, b_qkv, w_proj, bias_full):
    f32 = jnp.float32
    bf16 = jnp.bfloat16
    group, tok, feats = ln_w.shape
    heads = bias_full.shape[0]
    hdim = feats // heads
    scale = hdim ** (-0.5)
    qkv = jnp.einsum("gtc,cf->gtf", ln_w, w_qkv, preferred_element_type=f32) + b_qkv
    qkv = qkv.astype(bf16).reshape(group, tok, 3, heads, hdim)
    query = qkv[:, :, 0].transpose(0, 2, 1, 3)
    keys = qkv[:, :, 1].transpose(0, 2, 1, 3)
    values = qkv[:, :, 2].transpose(0, 2, 1, 3)
    scores = (
        jnp.einsum("ghid,ghjd->ghij", query, keys, preferred_element_type=f32) * scale
        + bias_full[None]
    )
    allowed = (lab_w[:, :, None] == lab_w[:, None, :])[:, None]
    scores = jnp.where(allowed, scores, f32(-1e30))
    top = jnp.max(scores, -1, keepdims=True)
    expo = jnp.exp(scores - top)
    probs = expo / jnp.sum(expo, -1, keepdims=True)
    probs_b = probs.astype(bf16)
    attended = jnp.einsum("ghij,ghjd->ghid", probs_b, values, preferred_element_type=f32)
    attended = attended.transpose(0, 2, 1, 3).reshape(group, tok, feats).astype(bf16)
    grad_att = jnp.einsum("gtc,fc->gtf", dy_w, w_proj, preferred_element_type=f32).astype(bf16)
    proj_part = jnp.einsum("gtf,gtc->fc", attended, dy_w, preferred_element_type=f32)
    grad_heads = grad_att.reshape(group, tok, heads, hdim).transpose(0, 2, 1, 3)
    grad_probs = jnp.einsum("ghid,ghjd->ghij", grad_heads, values, preferred_element_type=f32)
    grad_v = jnp.einsum("ghij,ghid->ghjd", probs_b, grad_heads, preferred_element_type=f32)
    grad_scores = probs * (grad_probs - jnp.sum(probs * grad_probs, -1, keepdims=True))
    rel_part = jnp.sum(grad_scores, 0)
    scores_b = grad_scores.astype(bf16)
    grad_q = jnp.einsum("ghij,ghjd->ghid", scores_b, keys, preferred_element_type=f32) * scale
    grad_k = jnp.einsum("ghij,ghid->ghjd", scores_b, query, preferred_element_type=f32) * scale
    grad_qkv = (
        jnp.stack([grad_q, grad_k, grad_v], 1)
        .transpose(0, 3, 1, 2, 4)
        .reshape(group, tok, 3 * feats)
    )
    bias_part = jnp.sum(grad_qkv, (0, 1))
    qkv_b = grad_qkv.astype(bf16)
    weight_part = jnp.einsum("gtc,gtf->cf", ln_w, qkv_b, preferred_element_type=f32)
    grad_in = jnp.einsum("gtf,cf->gtc", qkv_b, w_qkv, preferred_element_type=f32)
    return (grad_in, (weight_part, bias_part, proj_part, rel_part))


def shards(inputs, d_out, layer_norm_gain, layer_norm_bias, w_qkv, b_qkv, w_proj, rel_bias):
    f32 = jnp.float32
    cells_x, cells_y, cells_z, feats = inputs.shape
    tok = WIN**3
    heads = rel_bias.shape[0]
    xf = inputs.astype(f32)
    centered_input = xf - jnp.mean(xf, -1, keepdims=True)
    inverse_deviation = lax.rsqrt(
        jnp.mean(centered_input * centered_input, -1, keepdims=True) + 1e-05
    )
    normalized_input = centered_input * inverse_deviation
    normalized_tokens = (normalized_input * layer_norm_gain + layer_norm_bias).astype(jnp.bfloat16)
    moved_pair = jnp.stack([normalized_tokens, d_out])
    forward_steps = (forward_depth, forward_height, forward_width)
    backward_steps = (backward_depth, backward_height, backward_width)
    for advance in forward_steps:
        moved_pair = advance(moved_pair)
    label_x = region_label(lax.axis_index("gx") * cells_x, cells_x, cells_x * lax.axis_size("gx"))
    label_y = region_label(lax.axis_index("gy") * cells_y, cells_y, cells_y * lax.axis_size("gy"))
    label_z = region_label(lax.axis_index("gz") * cells_z, cells_z, cells_z * lax.axis_size("gz"))
    labels = label_x[:, None, None] * 9 + label_y[None, :, None] * 3 + label_z[None, None, :]
    bias_full = expand_table(rel_bias, WIN)
    group = cells_y // WIN * (cells_z // WIN)
    win_ln = to_windows(moved_pair[0]).reshape(-1, group, tok, feats)
    win_dy = to_windows(moved_pair[1]).reshape(-1, group, tok, feats)
    win_lab = to_windows(labels).reshape(-1, group, tok)

    def step(carry, item):
        grad_in, parts = window_pass(item[0], item[1], item[2], w_qkv, b_qkv, w_proj, bias_full)
        return (tuple((total + part for total, part in zip(carry, parts))), grad_in)

    start = (
        jnp.zeros((feats, 3 * feats), f32),
        jnp.zeros((3 * feats,), f32),
        jnp.zeros((feats, feats), f32),
        jnp.zeros((heads, tok, tok), f32),
    )
    sums, grad_win = lax.scan(step, start, (win_ln, win_dy, win_lab))
    normalized_output_gradient = from_windows(
        grad_win.reshape(-1, tok, feats), cells_x, cells_y, cells_z
    )
    for retreat in backward_steps:
        normalized_output_gradient = retreat(normalized_output_gradient)
    normalized_gradient = normalized_output_gradient * layer_norm_gain
    input_gradient_norm = inverse_deviation * (
        normalized_gradient
        - jnp.mean(normalized_gradient, -1, keepdims=True)
        - normalized_input * jnp.mean(normalized_gradient * normalized_input, -1, keepdims=True)
    )
    d_x = (d_out.astype(f32) + input_gradient_norm).astype(jnp.bfloat16)
    rel_local = fold_table(sums[3], WIN)
    local_gain = jnp.sum(normalized_output_gradient * normalized_input, (0, 1, 2))
    shift_local = jnp.sum(normalized_output_gradient, (0, 1, 2))
    totals = lax.psum(
        (sums[0], sums[1], sums[2], rel_local, local_gain, shift_local), ("gx", "gy", "gz")
    )
    count = (
        cells_x
        * cells_y
        * cells_z
        * lax.axis_size("gx")
        * lax.axis_size("gy")
        * lax.axis_size("gz")
    )
    inverse_width_factor = float(count) ** (-0.5)
    return (
        d_x,
        totals[0] * inverse_width_factor,
        totals[1] * inverse_width_factor,
        totals[2] * inverse_width_factor,
        totals[3] * inverse_width_factor,
        totals[4] * inverse_width_factor,
        totals[5] * inverse_width_factor,
    )


def solution(mesh):
    placed = (P("gx", "gy", "gz", None), P("gx", "gy", "gz", None), P(), P(), P(), P(), P(), P())
    return jax.shard_map(
        shards,
        mesh=mesh,
        in_specs=placed,
        out_specs=(P("gx", "gy", "gz", None), P(), P(), P(), P(), P(), P()),
        check_vma=False,
    )
```

profile of v0, /device:TPU:0, one launch (start us, length us, event | category | flops | bytes accessed | tf_op | source)
XLA Modules:
  0.0 697.9 jit_solution(15601233751291478034)
XLA Ops:
  7.2 2.4 convert_reduce_fusion
  15.1 5.1 collective-permute-start
  21.9 9.5 %convolution_bitcast_fusion.5 = f32[3,13,7,7,7,7]{1,2,5,3,0,4:T(8,128)S(1)} fusion(f32[3,13,13,7,7]{2,3,1,0,4:T(8,128)S(1)} %convolution_bitcast_fusion.7, s32[7,7]{0,1:T(8,128)S(1)} %subtract_add_fusion), kind=kOutput, calls=%fused_computation.96 | convolution fusion | flops 14608321 | bytes 474124 | tf_op jit(solution)/shard_map/hxycC,bBy->hxbcBC/dot_general | solution.py:30
  32.4 18.0 %collective-permute-start.1 = (bf16[2,28,3,7,96]{4,3,2,1,0:T(8,128)(2,1)S(1)}, bf16[2,28,3,7,96]{4,3,2,1,0:T(8,128)(2,1)S(1)}, u32[]{:S(2)}, u32[]{:S(2)}) collective-permute-start(bf16[2,28,3,7,96]{4,3,2,1,0:T(8,128)(2,1)S(1)} %pad_maximum_fusion.5), channel_id=1, source_target_pairs={{2,0},{4,2},{6,4},{0,6},{3,1},{5,3},{7,5},{1,7},{10,8},{12,10},{14... | collective-permute-start | bytes 677384 | tf_op jit(solution)/shard_map/ppermute | solution.py:13
  51.3 3.9 collective-permute-done.1
  56.1 2.9 copy.74
  60.5 71.1 %convolution_bitcast_fusion.3 = f32[3,7,7,7,7,7,7]{6,4,5,3,2,0,1:T(8,128)} fusion(f32[3,13,7,7,7,7]{1,2,5,3,0,4:T(8,128)S(1)} %convolution_bitcast_fusion.5, pred[7,7,13,1,1,1,1]{2,0,1,6,5,4,3:T(8,128)(4,1)S(1)} %fusion.73), kind=kOutput, calls=%fused_computation.61 | convolution fusion | flops 55059736 | bytes 1786981 | tf_op jit(solution)/shard_map/hxbcBC,aAx->habcABC/dot_general | solution.py:31
  131.7 59.5 %copy.82 = f32[3,7,7,7,7,7,7]{3,2,1,6,5,4,0:T(8,128)} copy(f32[3,7,7,7,7,7,7]{6,4,5,3,2,0,1:T(8,128)} %convolution_bitcast_fusion.3) | data formatting | bytes 2823576
  191.2 20.9 %add.240 = f32[3,343,343]{1,2,0:T(8,128)} reshape(f32[3,7,7,7,7,7,7]{3,2,1,6,5,4,0:T(8,128)} %copy.82) | data formatting | bytes 2823576 | tf_op jit(solution)/shard_map/while/body/eval_jaxpr/add | solution.py:113
  213.2 2.6 fusion.67
  217.5 2.1 pad_maximum_fusion.2
  221.5 2.5 copy.81
  225.9 2.5 copy.83
  228.5 134.0 %while.20 = (s32[]{:T(128)}, f32[96,288]{1,0:T(8,128)}, f32[288]{0:T(512)S(1)}, f32[96,96]{1,0:T(8,128)S(1)}, f32[3,343,343]{1,2,0:T(8,128)}, /*index=5*/f32[4,4...) while((s32[]{:T(128)}, f32[96,288]{1,0:T(8,128)}, ...), condition=%wide.wide.region_8.9_spmd.clone, body=%wide.wide.region_2.8_spmd.clone.sunk | while | flops 848489408 | bytes 107633568 | solution.py:183
  231.1 7.0 fusion.174
  238.3 6.9 multiply_reduce_fusion.4
  245.2 4.2 fusion.176
  253.8 2.1 fusion.180
  257.2 3.6 fusion.182
  263.4 7.0 fusion.174
  270.7 6.9 multiply_reduce_fusion.4
  277.6 4.2 fusion.176
  286.2 2.1 fusion.180
  288.3 2.7 select_add_fusion.7
  291.0 3.6 fusion.182
  297.2 7.0 fusion.174
  304.5 6.9 multiply_reduce_fusion.4
  311.4 4.2 fusion.176
  320.0 2.1 fusion.180
  322.1 2.7 select_add_fusion.7
  324.8 3.6 fusion.182
  331.0 7.0 fusion.174
  338.3 6.9 multiply_reduce_fusion.4
  345.2 4.2 fusion.176
  353.8 2.1 fusion.180
  355.9 2.7 select_add_fusion.7
  358.6 3.6 fusion.182
  362.5 3.4 copy.84
  368.9 20.0 %reshape.160 = f32[3,7,7,7,7,7,7]{3,2,1,6,5,4,0:T(8,128)} reshape(f32[3,343,343]{1,2,0:T(8,128)S(1)} %copy-done) | data formatting | bytes 2823576 | tf_op jit(solution)/shard_map/reshape | solution.py:39
  388.9 59.6 %copy.88 = f32[3,7,7,7,7,7,7]{1,6,4,5,3,2,0:T(8,128)} copy(f32[3,7,7,7,7,7,7]{3,2,1,6,5,4,0:T(8,128)} %reshape.160) | data formatting | bytes 2823576 | tf_op jit(solution)/shard_map/reshape | solution.py:39
  450.1 25.1 %convolution_bitcast_fusion.4 = f32[3,13,7,7,7,7]{1,5,4,3,2,0:T(8,128)} fusion(f32[3,7,7,7,7,7,7]{1,6,4,5,3,2,0:T(8,128)} %copy.88, s32[7,7]{0,1:T(8,128)S(1)} %copy-done.22), kind=kOutput, calls=%fused_computation.95 | convolution fusion | flops 55060372 | bytes 1786540 | tf_op jit(solution)/shard_map/habcABC,aAx->hxbcBC/dot_general | solution.py:40
  475.2 12.8 %copy.89 = f32[3,13,7,7,7,7]{2,3,4,5,1,0:T(8,128)} copy(f32[3,13,7,7,7,7]{1,5,4,3,2,0:T(8,128)} %convolution_bitcast_fusion.4) | data formatting | bytes 749112 | tf_op jit(solution)/shard_map/habcABC,aAx->hxbcBC/transpose | solution.py:40
  493.0 5.4 convolution_bitcast_fusion.6
  499.7 121.2 %all-reduce.3.cloned.1.call-done = f32[96,288]{1,0:T(8,128)} async-done(((f32[96,288]{1,0:T(8,128)}), f32[96,288]{1,0:T(8,128)}) %all-reduce.3.cloned.1.call-update) | async-done | bytes 110608 | tf_op jit(solution)/shard_map/psum | solution.py:199
  622.5 3.9 slice_reduce_fusion
  628.2 5.9 fusion.61
  634.2 43.7 %all-reduce = (f32[288]{0:T(512)S(1)}, f32[96,96]{1,0:T(8,128)S(1)}, f32[3,2197]{1,0:T(4,128)S(1)}, f32[96]{0:T(128)S(1)}, f32[96]{0:T(128)S(1)}) all-reduce(f32[288]{0:T(512)S(1)} %get-tuple-element.80, f32[96,96]{1,0:T(8,128)S(1)} %get-tuple-element.81, ...), channel_id=1, replica_groups=mesh['gx'=4,'gy'=4,'gz'=2] {'gx','gy','gz'}, use_global_device_ids=true, to_apply=%region_12.13 | all-reduce | flops 16287 | bytes 130296 | tf_op jit(solution)/shard_map/psum | solution.py:199
  682.9 8.0 %fusion.60 = bf16[28,28,7,96]{3,2,1,0:T(8,128)(2,1)} fusion(bf16[28,28,7,96]{3,2,1,0:T(8,128)(2,1)S(1)} %copy-done.2, bf16[28,28,7,96]{3,2,1,0:T(8,128)(2,1)S(1)} %copy-done.6, f32[28,28,7]{2,1,0:T(8,128)S(1)} %broadcast_multiply_fusion, f32[28,28,7]{2,1,0:T(8,128)S(1)} %broadcast_multiply_fusion.1, f32[96]{0:T(128)S(1)} %copy-done.26, ...), kind=kLoop, calls=%fused_computation.78 | loop fusion | flops 6322176 | bytes 5356672 | tf_op jit(solution)/shard_map/convert_element_type | solution.py:195
  (214 shorter events, 66.8 us)
Async XLA Ops:
  7.2 4.6 copy-start.25
  7.2 4.6 copy-start.27
  7.2 613.7 %all-reduce.3.cloned.1.call-start = ((), (), s32[]{:S(2)}) async-start(), calls=%async_computation | async-start | bytes 294912 | tf_op jit(solution)/shard_map/psum | solution.py:199
  9.8 4.1 copy-start.16
  9.8 5.2 copy-start.5
  13.8 6.4 copy-start.24
  15.1 17.2 %collective-permute-start = (bf16[2,3,28,7,96]{4,3,2,1,0:T(8,128)(2,1)S(1)}, bf16[2,3,28,7,96]{4,3,2,1,0:T(8,128)(2,1)S(1)}, u32[]{:S(2)}, u32[]{:S(2)}) collective-permute-start(bf16[2,3,28,7,96]{4,3,2,1,0:T(8,128)(2,1)S(1)} %pad_maximum_fusion.6), channel_id=1, source_target_pairs={{8,0},{16,8},{24,16},{0,24},{9,1},{17,9},{25,17},{1,25},{10,2},{18... | collective-permute-start | bytes 677384 | tf_op jit(solution)/shard_map/ppermute | solution.py:13
  20.2 30.2 %copy-start.21 = (s32[7,7]{0,1:T(8,128)}, s32[7,7]{0,1:T(8,128)S(1)}, u32[]{:S(2)}) copy-start(s32[7,7]{0,1:T(8,128)S(1)} %subtract_add_fusion) | copy-start | bytes 592
  20.5 11.0 %copy-start.12 = (bf16[1,28,28,7,96]{4,3,2,1,0:T(8,128)(2,1)S(1)}, bf16[1,28,28,7,96]{4,3,2,1,0:T(8,128)(2,1)}, u32[]{:S(2)}) copy-start(bf16[1,28,28,7,96]{4,3,2,1,0:T(8,128)(2,1)} %copy-done.11) | copy-start | bytes 3161092
  32.4 22.8 %collective-permute-start.1 = (bf16[2,28,3,7,96]{4,3,2,1,0:T(8,128)(2,1)S(1)}, bf16[2,28,3,7,96]{4,3,2,1,0:T(8,128)(2,1)S(1)}, u32[]{:S(2)}, u32[]{:S(2)}) collective-permute-start(bf16[2,28,3,7,96]{4,3,2,1,0:T(8,128)(2,1)S(1)} %pad_maximum_fusion.5), channel_id=1, source_target_pairs={{2,0},{4,2},{6,4},{0,6},{3,1},{5,3},{7,5},{1,7},{10,8},{12,10},{14... | collective-permute-start | bytes 677384 | tf_op jit(solution)/shard_map/ppermute | solution.py:13
  55.2 3.7 copy-start.19
  59.0 156.9 %collective-permute-start.2 = (bf16[2,28,28,3,96]{4,0,3,2,1:T(2,128)(2,1)}, bf16[2,28,28,3,96]{4,0,3,2,1:T(2,128)(2,1)}, u32[]{:S(2)}, u32[]{:S(2)}) collective-permute-start(bf16[2,28,28,3,96]{4,0,3,2,1:T(2,128)(2,1)} %copy.74), channel_id=1, source_target_pairs={{1,0},{0,1},{3,2},{2,3},{5,4},{4,5},{7,6},{6,7},{9,8},{8,9},{11,10... | collective-permute-start | bytes 2709512 | tf_op jit(solution)/shard_map/ppermute | solution.py:13
  224.0 4.5 copy-start.17
  224.0 4.5 copy-start.20
  224.1 4.4 copy-start.23
  228.7 9.3 %copy-start.9 = (bf16[4,4,343,96]{2,3,1,0:T(8,128)(2,1)}, bf16[4,4,343,96]{2,3,1,0:T(8,128)(2,1)S(1)}, u32[]{:S(2)}) copy-start(bf16[4,4,343,96]{2,3,1,0:T(8,128)(2,1)S(1)} %get-tuple-element.416) | copy-start | bytes 3161092 | tf_op jit(solution)/shard_map/while
  228.7 9.3 %copy-start.13 = (bf16[4,4,343,96]{2,3,1,0:T(8,128)(2,1)}, bf16[4,4,343,96]{2,3,1,0:T(8,128)(2,1)S(1)}, u32[]{:S(2)}) copy-start(bf16[4,4,343,96]{2,3,1,0:T(8,128)(2,1)S(1)} %get-tuple-element.421) | copy-start | bytes 3161092 | tf_op jit(solution)/shard_map/while
  238.3 6.9 slice-start
  238.3 6.9 slice-start.1
  257.2 3.6 copy-start.14
  257.2 3.8 copy-start.10
  261.1 9.3 %copy-start.9 = (bf16[4,4,343,96]{2,3,1,0:T(8,128)(2,1)}, bf16[4,4,343,96]{2,3,1,0:T(8,128)(2,1)S(1)}, u32[]{:S(2)}) copy-start(bf16[4,4,343,96]{2,3,1,0:T(8,128)(2,1)S(1)} %get-tuple-element.416) | copy-start | bytes 3161092 | tf_op jit(solution)/shard_map/while
  261.1 9.3 %copy-start.13 = (bf16[4,4,343,96]{2,3,1,0:T(8,128)(2,1)}, bf16[4,4,343,96]{2,3,1,0:T(8,128)(2,1)S(1)}, u32[]{:S(2)}) copy-start(bf16[4,4,343,96]{2,3,1,0:T(8,128)(2,1)S(1)} %get-tuple-element.421) | copy-start | bytes 3161092 | tf_op jit(solution)/shard_map/while
  270.7 6.9 slice-start
  270.7 6.9 slice-start.1
  291.0 3.8 copy-start.10
  294.9 9.3 %copy-start.9 = (bf16[4,4,343,96]{2,3,1,0:T(8,128)(2,1)}, bf16[4,4,343,96]{2,3,1,0:T(8,128)(2,1)S(1)}, u32[]{:S(2)}) copy-start(bf16[4,4,343,96]{2,3,1,0:T(8,128)(2,1)S(1)} %get-tuple-element.416) | copy-start | bytes 3161092 | tf_op jit(solution)/shard_map/while
  294.9 9.3 %copy-start.13 = (bf16[4,4,343,96]{2,3,1,0:T(8,128)(2,1)}, bf16[4,4,343,96]{2,3,1,0:T(8,128)(2,1)S(1)}, u32[]{:S(2)}) copy-start(bf16[4,4,343,96]{2,3,1,0:T(8,128)(2,1)S(1)} %get-tuple-element.421) | copy-start | bytes 3161092 | tf_op jit(solution)/shard_map/while
  304.4 6.9 slice-start
  304.4 6.9 slice-start.1
  324.8 3.6 copy-start.14
  324.8 3.8 copy-start.10
  328.7 9.3 %copy-start.9 = (bf16[4,4,343,96]{2,3,1,0:T(8,128)(2,1)}, bf16[4,4,343,96]{2,3,1,0:T(8,128)(2,1)S(1)}, u32[]{:S(2)}) copy-start(bf16[4,4,343,96]{2,3,1,0:T(8,128)(2,1)S(1)} %get-tuple-element.416) | copy-start | bytes 3161092 | tf_op jit(solution)/shard_map/while
  328.7 9.3 %copy-start.13 = (bf16[4,4,343,96]{2,3,1,0:T(8,128)(2,1)}, bf16[4,4,343,96]{2,3,1,0:T(8,128)(2,1)S(1)}, u32[]{:S(2)}) copy-start(bf16[4,4,343,96]{2,3,1,0:T(8,128)(2,1)S(1)} %get-tuple-element.421) | copy-start | bytes 3161092 | tf_op jit(solution)/shard_map/while
  338.3 6.9 slice-start
  338.3 6.9 slice-start.1
  358.6 3.6 copy-start.14
  358.6 3.8 copy-start.10
  367.1 81.4 %collective-permute-start.3 = (f32[3,28,7,96]{3,2,1,0:T(8,128)}, f32[3,28,7,96]{3,2,1,0:T(8,128)S(1)}, u32[]{:S(2)}, u32[]{:S(2)}) collective-permute-start(f32[3,28,7,96]{3,2,1,0:T(8,128)} %slice.79), channel_id=1, source_target_pairs={{24,0},{0,8},{8,16},{16,24},{25,1},{1,9},{9,17},{17,25},{26,2},{2,... | collective-permute-start | bytes 677384 | tf_op jit(solution)/shard_map/ppermute | solution.py:13
  388.9 59.6 %copy-start.4 = (f32[25,28,7,96]{3,2,1,0:T(8,128)S(1)}, f32[25,28,7,96]{3,2,1,0:T(8,128)}, u32[]{:S(2)}) copy-start(f32[25,28,7,96]{3,2,1,0:T(8,128)} %slice.80) | copy-start | bytes 5644804
  449.3 38.7 %collective-permute-start.4 = (f32[28,3,7,96]{3,2,1,0:T(8,128)}, f32[28,3,7,96]{3,2,1,0:T(8,128)}, u32[]{:S(2)}, u32[]{:S(2)}) collective-permute-start(f32[28,3,7,96]{3,2,1,0:T(8,128)} %pad_maximum_fusion.4), channel_id=1, source_target_pairs={{6,0},{0,2},{2,4},{4,6},{7,1},{1,3},{3,5},{5,7},{14,8},{8,10},{10,... | collective-permute-start | bytes 677384 | tf_op jit(solution)/shard_map/ppermute | solution.py:13
  488.0 5.0 copy-start.3
  489.6 8.8 %copy-start.15 = (f32[28,28,7,96]{3,2,1,0:T(8,128)}, f32[28,28,7,96]{3,2,1,0:T(8,128)S(1)}, u32[]{:S(2)}) copy-start(f32[28,28,7,96]{3,2,1,0:T(8,128)S(1)} %fusion.63) | copy-start | bytes 6322180
  491.3 135.1 %collective-permute-start.5 = (f32[28,28,3,96]{3,1,2,0:T(8,128)}, f32[28,28,3,96]{3,1,2,0:T(8,128)S(1)}, u32[]{:S(2)}, u32[]{:S(2)}) collective-permute-start(f32[28,28,3,96]{3,1,2,0:T(8,128)} %copy.86), channel_id=1, source_target_pairs={{1,0},{0,1},{3,2},{2,3},{5,4},{4,5},{7,6},{6,7},{9,8},{8,9},{11,10... | collective-permute-start | bytes 2709512 | tf_op jit(solution)/shard_map/ppermute | solution.py:13
  622.5 5.3 copy-start.2
  622.5 5.3 copy-start.26
  627.8 6.4 copy-start.8
  628.2 54.6 %copy-start.6 = (bf16[28,28,7,96]{3,2,1,0:T(8,128)(2,1)S(1)}, bf16[28,28,7,96]{3,2,1,0:T(8,128)(2,1)}, u32[]{:S(2)}) copy-start(bf16[28,28,7,96]{3,2,1,0:T(8,128)(2,1)} %param.11) | copy-start | bytes 3161092
  (7 other events, 16.2 us)
Sparse Core Ops, SparseCore 0:
  498.6 122.2 all-reduce.2
where the time goes:
time: 706 us; the launch traced here: 698 us
  matrix products  211 us (30%)
  local copies, waits for them, and re-layouts  203 us (29%)
  waiting for transfers between devices  125 us (18%)
  other arithmetic  73.7 us (10%)
  blocking collectives  43.7 us (6%)
  starting transfers between devices  26.1 us (4%)
  between operations  14.7 us (2%)
    psum x1, waiting for transfers between devices, shards(): lax.psum((sums[0], sums[1], sums[2], rel_local, local_gain, shift_local),...  121 us
    reshape x2, local copies, waits for them, and re-layouts, fold_table(): grid = pairs.reshape(heads, span, span, span, span, span, span)  79.7 us
    dot_general x1, matrix products, expand_table(): section = jnp.einsum('hxbcBC,aAx->habcABC', section, ones, precision=exact)  71.1 us
    unnamed x51, local copies, waits for them, and re-layouts  67.5 us
    psum x1, blocking collectives, shards(): lax.psum((sums[0], sums[1], sums[2], rel_local, local_gain, shift_local),...  43.7 us
    sub x4, matrix products, window_pass(): expo = jnp.exp(scores - top)  27.8 us
    dot_general x4, matrix products, window_pass(): jnp.einsum('ghid,ghjd->ghij', grad_heads, values, preferred_element_type=...  27.7 us
    ppermute x6, starting transfers between devices, shifted(): return lax.ppermute(block, axis, route)  26 us
  transfers between devices with their start and end apart: 7, of which 2 were waited for; matrix products, arithmetic and copies ran while one was open for 43% of the time, Pallas kernels for 0%

commit v1 on v0

--- a/solution.py
+++ b/solution.py
@@ -197,7 +197,8 @@
     local_gain = jnp.sum(normalized_output_gradient * normalized_input, (0, 1, 2))
     shift_local = jnp.sum(normalized_output_gradient, (0, 1, 2))
     totals = lax.psum(
-        (sums[0], sums[1], sums[2], rel_local, local_gain, shift_local), ("gx", "gy", "gz")
+        lax.psum((sums[0], sums[1], sums[2], rel_local, local_gain, shift_local), ("gy", "gz")),
+        "gx",
     )
     count = (
         cells_x

time: 706 us -> 664 us (0.941)
  waiting for transfers between devices: 125 us -> 81.8 us
    psum x1, waiting for transfers between devices: 121 us -> 41.5 us  [shards(): lax.psum((sums[0], sums[1], sums[2], rel_local, local_gain, shift_local),...]
    psum x0 -> x1, waiting for transfers between devices: none -> 36.3 us  [shards(): lax.psum(lax.psum((sums[0], sums[1], sums[2], rel_local, local_gain, shif...]
    psum x0 -> x1, blocking collectives: none -> 19.3 us  [shards(): lax.psum(lax.psum((sums[0], sums[1], sums[2], rel_local, local_gain, shif...]
    psum x1, blocking collectives: 43.7 us -> 25.5 us  [shards(): lax.psum((sums[0], sums[1], sums[2], rel_local, local_gain, shift_local),...]
  transfers between devices with their start and end apart: 7 -> 8, of which waited for: 2 -> 3; matrix products, arithmetic and copies ran while one was open for 43% -> 46% of each run, Pallas kernels for 0% -> 0%
where the time goes in v1:
time: 664 us; the launch traced here: 656 us
  matrix products  210 us (32%)
  local copies, waits for them, and re-layouts  204 us (31%)
  waiting for transfers between devices  81.8 us (12%)
  other arithmetic  73.7 us (11%)
  blocking collectives  44.8 us (7%)
  starting transfers between devices  26.3 us (4%)
  between operations  14.8 us (2%)
    reshape x2, local copies, waits for them, and re-layouts, fold_table(): grid = pairs.reshape(heads, span, span, span, span, span, span)  79.8 us
    dot_general x1, matrix products, expand_table(): section = jnp.einsum('hxbcBC,aAx->habcABC', section, ones, precision=exact)  71.1 us
    unnamed x51, local copies, waits for them, and re-layouts  68.1 us
    psum x1, waiting for transfers between devices, shards(): lax.psum((sums[0], sums[1], sums[2], rel_local, local_gain, shift_local),...  41.5 us
    psum x1, waiting for transfers between devices, shards(): lax.psum(lax.psum((sums[0], sums[1], sums[2], rel_local, local_gain, shif...  36.3 us
    sub x4, matrix products, window_pass(): expo = jnp.exp(scores - top)  27.7 us
    dot_general x4, matrix products, window_pass(): jnp.einsum('ghid,ghjd->ghij', grad_heads, values, preferred_element_type=...  27.6 us
    ppermute x6, starting transfers between devices, shifted(): return lax.ppermute(block, axis, route)  26 us
  transfers between devices with their start and end apart: 8, of which 3 were waited for; matrix products, arithmetic and copies ran while one was open for 46% of the time, Pallas kernels for 0%

profile of v1, /device:TPU:0, one launch (start us, length us, event | category | flops | bytes accessed | tf_op | source)
XLA Modules:
  0.0 656.2 jit_solution(4956379097109403098)
XLA Ops:
  7.2 2.4 convert_reduce_fusion
  15.1 5.1 collective-permute-start
  21.9 9.5 %convolution_bitcast_fusion.5 = f32[3,13,7,7,7,7]{1,2,5,3,0,4:T(8,128)S(1)} fusion(f32[3,13,13,7,7]{2,3,1,0,4:T(8,128)S(1)} %convolution_bitcast_fusion.7, s32[7,7]{0,1:T(8,128)S(1)} %subtract_add_fusion), kind=kOutput, calls=%fused_computation.96 | convolution fusion | flops 14608321 | bytes 474124 | tf_op jit(solution)/shard_map/hxycC,bBy->hxbcBC/dot_general | solution.py:30
  32.4 18.0 %collective-permute-start.1 = (bf16[2,28,3,7,96]{4,3,2,1,0:T(8,128)(2,1)S(1)}, bf16[2,28,3,7,96]{4,3,2,1,0:T(8,128)(2,1)S(1)}, u32[]{:S(2)}, u32[]{:S(2)}) collective-permute-start(bf16[2,28,3,7,96]{4,3,2,1,0:T(8,128)(2,1)S(1)} %pad_maximum_fusion.5), channel_id=1, source_target_pairs={{2,0},{4,2},{6,4},{0,6},{3,1},{5,3},{7,5},{1,7},{10,8},{12,10},{14... | collective-permute-start | bytes 677384 | tf_op jit(solution)/shard_map/ppermute | solution.py:13
  51.3 3.9 collective-permute-done.1
  56.1 2.9 copy.74
  60.5 71.1 %convolution_bitcast_fusion.3 = f32[3,7,7,7,7,7,7]{6,4,5,3,2,0,1:T(8,128)} fusion(f32[3,13,7,7,7,7]{1,2,5,3,0,4:T(8,128)S(1)} %convolution_bitcast_fusion.5, pred[7,7,13,1,1,1,1]{2,0,1,6,5,4,3:T(8,128)(4,1)S(1)} %fusion.73), kind=kOutput, calls=%fused_computation.61 | convolution fusion | flops 55059736 | bytes 1786981 | tf_op jit(solution)/shard_map/hxbcBC,aAx->habcABC/dot_general | solution.py:31
  131.6 59.5 %copy.82 = f32[3,7,7,7,7,7,7]{3,2,1,6,5,4,0:T(8,128)} copy(f32[3,7,7,7,7,7,7]{6,4,5,3,2,0,1:T(8,128)} %convolution_bitcast_fusion.3) | data formatting | bytes 2823576
  191.2 20.9 %add.252 = f32[3,343,343]{1,2,0:T(8,128)} reshape(f32[3,7,7,7,7,7,7]{3,2,1,6,5,4,0:T(8,128)} %copy.82) | data formatting | bytes 2823576 | tf_op jit(solution)/shard_map/while/body/eval_jaxpr/add | solution.py:113
  213.2 2.6 fusion.67
  221.5 2.5 copy.81
  225.9 2.5 copy.83
  228.5 133.8 %while.20 = (s32[]{:T(128)}, f32[96,288]{1,0:T(8,128)}, f32[288]{0:T(512)S(1)}, f32[96,96]{1,0:T(8,128)S(1)}, f32[3,343,343]{1,2,0:T(8,128)}, /*index=5*/f32[4,4...) while((s32[]{:T(128)}, f32[96,288]{1,0:T(8,128)}, ...), condition=%wide.wide.region_8.9_spmd.clone, body=%wide.wide.region_2.8_spmd.clone.sunk | while | flops 848489408 | bytes 107633568 | solution.py:183
  231.1 6.9 %fusion.174 = (f32[4,3,343]{2,1,0:T(4,128)S(1)}, f32[4,3,343,343]{2,3,1,0:T(8,128)}) fusion(f32[3,343,343]{1,2,0:T(8,128)} %get-tuple-element.428, pred[4,343,343]{1,2,0:T(8,128)(4,1)} %broadcast_compare_fusion.3, bf16[4,343,3,3,32]{1,4,3,2,0:T(8,128)(2,1)S(1)} %bitcast.281), kind=kOutput, calls=%fused_computation.146.clone.clone.1 | convolution fusion | flops 97413720 | bytes 8135824 | tf_op jit(solution)/shard_map/while/body/eval_jaxpr/sub | solution.py:119
  238.2 6.9 %multiply_reduce_fusion.4 = (f32[4,3,343]{2,1,0:T(4,128)S(1)}, f32[4,3,343,343]{2,3,1,0:T(8,128)}) fusion(f32[4,3,343,343]{2,3,1,0:T(8,128)} %get-tuple-element.377, f32[4,3,343]{2,1,0:T(4,128)S(1)} %get-tuple-element.378, bf16[4,3,343,32]{2,3,1,0:T(8,128)(2,1)S(1)} %bitcast.292, bf16[4,343,3,3,32]{1,4,3,2,0:T(8,128)(2,1)S(1)} %bitcast.282), kind=kOutput, calls=%fused_computation.2.clone.clone.1 | convolution fusion | flops 94585688 | bytes 11925168 | tf_op jit(solution)/shard_map/while/body/eval_jaxpr/ghid,ghjd->ghij/dot_general | solution.py:127
  245.2 4.2 fusion.176
  257.1 3.6 fusion.182
  263.3 6.9 %fusion.174 = (f32[4,3,343]{2,1,0:T(4,128)S(1)}, f32[4,3,343,343]{2,3,1,0:T(8,128)}) fusion(f32[3,343,343]{1,2,0:T(8,128)} %get-tuple-element.428, pred[4,343,343]{1,2,0:T(8,128)(4,1)} %broadcast_compare_fusion.3, bf16[4,343,3,3,32]{1,4,3,2,0:T(8,128)(2,1)S(1)} %bitcast.281), kind=kOutput, calls=%fused_computation.146.clone.clone.1 | convolution fusion | flops 97413720 | bytes 8135824 | tf_op jit(solution)/shard_map/while/body/eval_jaxpr/sub | solution.py:119
  270.6 6.9 %multiply_reduce_fusion.4 = (f32[4,3,343]{2,1,0:T(4,128)S(1)}, f32[4,3,343,343]{2,3,1,0:T(8,128)}) fusion(f32[4,3,343,343]{2,3,1,0:T(8,128)} %get-tuple-element.377, f32[4,3,343]{2,1,0:T(4,128)S(1)} %get-tuple-element.378, bf16[4,3,343,32]{2,3,1,0:T(8,128)(2,1)S(1)} %bitcast.292, bf16[4,343,3,3,32]{1,4,3,2,0:T(8,128)(2,1)S(1)} %bitcast.282), kind=kOutput, calls=%fused_computation.2.clone.clone.1 | convolution fusion | flops 94585688 | bytes 11925168 | tf_op jit(solution)/shard_map/while/body/eval_jaxpr/ghid,ghjd->ghij/dot_general | solution.py:127
  277.5 4.2 fusion.176
  286.1 2.1 fusion.180
  288.2 2.7 select_add_fusion.7
  290.9 3.6 fusion.182
  297.1 6.9 %fusion.174 = (f32[4,3,343]{2,1,0:T(4,128)S(1)}, f32[4,3,343,343]{2,3,1,0:T(8,128)}) fusion(f32[3,343,343]{1,2,0:T(8,128)} %get-tuple-element.428, pred[4,343,343]{1,2,0:T(8,128)(4,1)} %broadcast_compare_fusion.3, bf16[4,343,3,3,32]{1,4,3,2,0:T(8,128)(2,1)S(1)} %bitcast.281), kind=kOutput, calls=%fused_computation.146.clone.clone.1 | convolution fusion | flops 97413720 | bytes 8135824 | tf_op jit(solution)/shard_map/while/body/eval_jaxpr/sub | solution.py:119
  304.3 6.9 %multiply_reduce_fusion.4 = (f32[4,3,343]{2,1,0:T(4,128)S(1)}, f32[4,3,343,343]{2,3,1,0:T(8,128)}) fusion(f32[4,3,343,343]{2,3,1,0:T(8,128)} %get-tuple-element.377, f32[4,3,343]{2,1,0:T(4,128)S(1)} %get-tuple-element.378, bf16[4,3,343,32]{2,3,1,0:T(8,128)(2,1)S(1)} %bitcast.292, bf16[4,343,3,3,32]{1,4,3,2,0:T(8,128)(2,1)S(1)} %bitcast.282), kind=kOutput, calls=%fused_computation.2.clone.clone.1 | convolution fusion | flops 94585688 | bytes 11925168 | tf_op jit(solution)/shard_map/while/body/eval_jaxpr/ghid,ghjd->ghij/dot_general | solution.py:127
  311.3 4.2 fusion.176
  319.8 2.1 fusion.180
  322.0 2.7 select_add_fusion.7
  324.7 3.6 fusion.182
  330.9 6.9 %fusion.174 = (f32[4,3,343]{2,1,0:T(4,128)S(1)}, f32[4,3,343,343]{2,3,1,0:T(8,128)}) fusion(f32[3,343,343]{1,2,0:T(8,128)} %get-tuple-element.428, pred[4,343,343]{1,2,0:T(8,128)(4,1)} %broadcast_compare_fusion.3, bf16[4,343,3,3,32]{1,4,3,2,0:T(8,128)(2,1)S(1)} %bitcast.281), kind=kOutput, calls=%fused_computation.146.clone.clone.1 | convolution fusion | flops 97413720 | bytes 8135824 | tf_op jit(solution)/shard_map/while/body/eval_jaxpr/sub | solution.py:119
  338.1 6.9 %multiply_reduce_fusion.4 = (f32[4,3,343]{2,1,0:T(4,128)S(1)}, f32[4,3,343,343]{2,3,1,0:T(8,128)}) fusion(f32[4,3,343,343]{2,3,1,0:T(8,128)} %get-tuple-element.377, f32[4,3,343]{2,1,0:T(4,128)S(1)} %get-tuple-element.378, bf16[4,3,343,32]{2,3,1,0:T(8,128)(2,1)S(1)} %bitcast.292, bf16[4,343,3,3,32]{1,4,3,2,0:T(8,128)(2,1)S(1)} %bitcast.282), kind=kOutput, calls=%fused_computation.2.clone.clone.1 | convolution fusion | flops 94585688 | bytes 11925168 | tf_op jit(solution)/shard_map/while/body/eval_jaxpr/ghid,ghjd->ghij/dot_general | solution.py:127
  345.0 4.2 fusion.176
  353.6 2.1 fusion.180
  355.7 2.7 select_add_fusion.7
  358.5 3.6 fusion.182
  362.3 3.4 copy.84
  368.7 20.1 %reshape.160 = f32[3,7,7,7,7,7,7]{3,2,1,6,5,4,0:T(8,128)} reshape(f32[3,343,343]{1,2,0:T(8,128)S(1)} %copy-done) | data formatting | bytes 2823576 | tf_op jit(solution)/shard_map/reshape | solution.py:39
  388.7 59.7 %copy.88 = f32[3,7,7,7,7,7,7]{1,6,4,5,3,2,0:T(8,128)} copy(f32[3,7,7,7,7,7,7]{3,2,1,6,5,4,0:T(8,128)} %reshape.160) | data formatting | bytes 2823576 | tf_op jit(solution)/shard_map/reshape | solution.py:39
  450.1 25.0 %convolution_bitcast_fusion.4 = f32[3,13,7,7,7,7]{1,5,4,3,2,0:T(8,128)} fusion(f32[3,7,7,7,7,7,7]{1,6,4,5,3,2,0:T(8,128)} %copy.88, s32[7,7]{0,1:T(8,128)S(1)} %copy-done.22), kind=kOutput, calls=%fused_computation.95 | convolution fusion | flops 55060372 | bytes 1786540 | tf_op jit(solution)/shard_map/habcABC,aAx->hxbcBC/dot_general | solution.py:40
  475.1 12.7 %copy.89 = f32[3,13,7,7,7,7]{2,3,4,5,1,0:T(8,128)} copy(f32[3,13,7,7,7,7]{1,5,4,3,2,0:T(8,128)} %convolution_bitcast_fusion.4) | data formatting | bytes 749112 | tf_op jit(solution)/shard_map/habcABC,aAx->hxbcBC/transpose | solution.py:40
  493.6 5.4 convolution_bitcast_fusion.6
  499.0 41.5 %all-reduce.5.cloned.1.call-done = f32[96,288]{1,0:T(8,128)} async-done(((f32[96,288]{1,0:T(8,128)}), f32[96,288]{1,0:T(8,128)}) %all-reduce.5.cloned.1.call-update) | async-done | bytes 110608 | tf_op jit(solution)/shard_map/psum | solution.py:200
  541.8 36.3 %all-reduce.7.cloned.1.call-done = f32[96,288]{1,0:T(8,128)} async-done(((f32[96,288]{1,0:T(8,128)}), f32[96,288]{1,0:T(8,128)}) %all-reduce.7.cloned.1.call-update) | async-done | bytes 110608 | tf_op jit(solution)/shard_map/psum | solution.py:199
  579.7 4.0 slice_reduce_fusion
  585.4 5.9 fusion.61
  591.4 25.5 %all-reduce = (f32[288]{0:T(512)S(1)}, f32[96,96]{1,0:T(8,128)S(1)}, f32[3,2197]{1,0:T(4,128)S(1)}, f32[96]{0:T(128)S(1)}, f32[96]{0:T(128)S(1)}) all-reduce(f32[288]{0:T(512)S(1)} %get-tuple-element.80, f32[96,96]{1,0:T(8,128)S(1)} %get-tuple-element.81, ...), channel_id=1, replica_groups=mesh['gx'=4,'gy'=4,'gz'=2] {'gy','gz'}, use_global_device_ids=true, to_apply=%region_13.14 | all-reduce | flops 16287 | bytes 130296 | tf_op jit(solution)/shard_map/psum | solution.py:200
  616.9 19.3 %all-reduce.1 = (f32[288]{0:T(512)S(1)}, f32[96,96]{1,0:T(8,128)S(1)}, f32[3,2197]{1,0:T(4,128)S(1)}, f32[96]{0:T(128)S(1)}, f32[96]{0:T(128)S(1)}) all-reduce(f32[288]{0:T(512)S(1)} %get-tuple-element.206, f32[96,96]{1,0:T(8,128)S(1)} %get-tuple-element.207, ...), channel_id=1, replica_groups=mesh['gx'=4,'gy'=4,'gz'=2] {'gx'}, use_global_device_ids=true, to_apply=%region_14.15 | all-reduce | flops 16287 | bytes 130296 | tf_op jit(solution)/shard_map/psum | solution.py:199
  641.2 8.0 %fusion.60 = bf16[28,28,7,96]{3,2,1,0:T(8,128)(2,1)} fusion(bf16[28,28,7,96]{3,2,1,0:T(8,128)(2,1)S(1)} %copy-done.2, bf16[28,28,7,96]{3,2,1,0:T(8,128)(2,1)S(1)} %copy-done.6, f32[28,28,7]{2,1,0:T(8,128)S(1)} %broadcast_multiply_fusion, f32[28,28,7]{2,1,0:T(8,128)S(1)} %broadcast_multiply_fusion.1, f32[96]{0:T(128)S(1)} %copy-done.26, ...), kind=kLoop, calls=%fused_computation.78 | loop fusion | flops 6322176 | bytes 5356672 | tf_op jit(solution)/shard_map/convert_element_type | solution.py:195
  (218 shorter events, 71.7 us)
Async XLA Ops:
  7.2 4.6 copy-start.25
  7.2 4.6 copy-start.27
  7.2 533.3 %all-reduce.5.cloned.1.call-start = ((), (), s32[]{:S(2)}) async-start(), calls=%async_computation | async-start | bytes 294912 | tf_op jit(solution)/shard_map/psum | solution.py:200
  9.8 4.1 copy-start.16
  9.8 5.2 copy-start.5
  13.8 6.4 copy-start.24
  15.1 17.2 %collective-permute-start = (bf16[2,3,28,7,96]{4,3,2,1,0:T(8,128)(2,1)S(1)}, bf16[2,3,28,7,96]{4,3,2,1,0:T(8,128)(2,1)S(1)}, u32[]{:S(2)}, u32[]{:S(2)}) collective-permute-start(bf16[2,3,28,7,96]{4,3,2,1,0:T(8,128)(2,1)S(1)} %pad_maximum_fusion.6), channel_id=1, source_target_pairs={{8,0},{16,8},{24,16},{0,24},{9,1},{17,9},{25,17},{1,25},{10,2},{18... | collective-permute-start | bytes 677384 | tf_op jit(solution)/shard_map/ppermute | solution.py:13
  20.2 30.2 %copy-start.21 = (s32[7,7]{0,1:T(8,128)}, s32[7,7]{0,1:T(8,128)S(1)}, u32[]{:S(2)}) copy-start(s32[7,7]{0,1:T(8,128)S(1)} %subtract_add_fusion) | copy-start | bytes 592
  20.5 11.0 %copy-start.12 = (bf16[1,28,28,7,96]{4,3,2,1,0:T(8,128)(2,1)S(1)}, bf16[1,28,28,7,96]{4,3,2,1,0:T(8,128)(2,1)}, u32[]{:S(2)}) copy-start(bf16[1,28,28,7,96]{4,3,2,1,0:T(8,128)(2,1)} %copy-done.11) | copy-start | bytes 3161092
  32.4 22.8 %collective-permute-start.1 = (bf16[2,28,3,7,96]{4,3,2,1,0:T(8,128)(2,1)S(1)}, bf16[2,28,3,7,96]{4,3,2,1,0:T(8,128)(2,1)S(1)}, u32[]{:S(2)}, u32[]{:S(2)}) collective-permute-start(bf16[2,28,3,7,96]{4,3,2,1,0:T(8,128)(2,1)S(1)} %pad_maximum_fusion.5), channel_id=1, source_target_pairs={{2,0},{4,2},{6,4},{0,6},{3,1},{5,3},{7,5},{1,7},{10,8},{12,10},{14... | collective-permute-start | bytes 677384 | tf_op jit(solution)/shard_map/ppermute | solution.py:13
  55.2 3.7 copy-start.19
  59.0 156.9 %collective-permute-start.2 = (bf16[2,28,28,3,96]{4,0,3,2,1:T(2,128)(2,1)}, bf16[2,28,28,3,96]{4,0,3,2,1:T(2,128)(2,1)}, u32[]{:S(2)}, u32[]{:S(2)}) collective-permute-start(bf16[2,28,28,3,96]{4,0,3,2,1:T(2,128)(2,1)} %copy.74), channel_id=1, source_target_pairs={{1,0},{0,1},{3,2},{2,3},{5,4},{4,5},{7,6},{6,7},{9,8},{8,9},{11,10... | collective-permute-start | bytes 2709512 | tf_op jit(solution)/shard_map/ppermute | solution.py:13
  224.0 4.5 copy-start.17
  224.0 4.5 copy-start.20
  224.1 4.5 copy-start.23
  228.7 9.3 %copy-start.9 = (bf16[4,4,343,96]{2,3,1,0:T(8,128)(2,1)}, bf16[4,4,343,96]{2,3,1,0:T(8,128)(2,1)S(1)}, u32[]{:S(2)}) copy-start(bf16[4,4,343,96]{2,3,1,0:T(8,128)(2,1)S(1)} %get-tuple-element.421) | copy-start | bytes 3161092 | tf_op jit(solution)/shard_map/while
  228.7 9.3 %copy-start.13 = (bf16[4,4,343,96]{2,3,1,0:T(8,128)(2,1)}, bf16[4,4,343,96]{2,3,1,0:T(8,128)(2,1)S(1)}, u32[]{:S(2)}) copy-start(bf16[4,4,343,96]{2,3,1,0:T(8,128)(2,1)S(1)} %get-tuple-element.426) | copy-start | bytes 3161092 | tf_op jit(solution)/shard_map/while
  238.2 6.9 %slice-start = ((s8[6340608]{0:T(1024)(128)(4,1)}), s8[4194304]{0:T(1024)(128)(4,1)S(1)}, s32[]{:S(2)}) async-start(s8[6340608]{0:T(1024)(128)(4,1)} %bitcast.279), calls=%async_computation.2 | async-start | bytes 8388608 | tf_op jit(solution)/shard_map/while
  238.2 6.9 %slice-start.1 = ((s8[6340608]{0:T(1024)(128)(4,1)}), s8[2146304]{0:T(1024)(128)(4,1)S(1)}, s32[]{:S(2)}) async-start(s8[6340608]{0:T(1024)(128)(4,1)} %bitcast.279), calls=%async_computation.3 | async-start | bytes 4292608 | tf_op jit(solution)/shard_map/while
  257.1 3.6 copy-start.14
  257.1 3.8 copy-start.10
  261.0 9.3 %copy-start.9 = (bf16[4,4,343,96]{2,3,1,0:T(8,128)(2,1)}, bf16[4,4,343,96]{2,3,1,0:T(8,128)(2,1)S(1)}, u32[]{:S(2)}) copy-start(bf16[4,4,343,96]{2,3,1,0:T(8,128)(2,1)S(1)} %get-tuple-element.421) | copy-start | bytes 3161092 | tf_op jit(solution)/shard_map/while
  261.0 9.3 %copy-start.13 = (bf16[4,4,343,96]{2,3,1,0:T(8,128)(2,1)}, bf16[4,4,343,96]{2,3,1,0:T(8,128)(2,1)S(1)}, u32[]{:S(2)}) copy-start(bf16[4,4,343,96]{2,3,1,0:T(8,128)(2,1)S(1)} %get-tuple-element.426) | copy-start | bytes 3161092 | tf_op jit(solution)/shard_map/while
  270.5 6.9 %slice-start = ((s8[6340608]{0:T(1024)(128)(4,1)}), s8[4194304]{0:T(1024)(128)(4,1)S(1)}, s32[]{:S(2)}) async-start(s8[6340608]{0:T(1024)(128)(4,1)} %bitcast.279), calls=%async_computation.2 | async-start | bytes 8388608 | tf_op jit(solution)/shard_map/while
  270.5 6.9 %slice-start.1 = ((s8[6340608]{0:T(1024)(128)(4,1)}), s8[2146304]{0:T(1024)(128)(4,1)S(1)}, s32[]{:S(2)}) async-start(s8[6340608]{0:T(1024)(128)(4,1)} %bitcast.279), calls=%async_computation.3 | async-start | bytes 4292608 | tf_op jit(solution)/shard_map/while
  290.9 3.8 copy-start.10
  294.8 9.3 %copy-start.9 = (bf16[4,4,343,96]{2,3,1,0:T(8,128)(2,1)}, bf16[4,4,343,96]{2,3,1,0:T(8,128)(2,1)S(1)}, u32[]{:S(2)}) copy-start(bf16[4,4,343,96]{2,3,1,0:T(8,128)(2,1)S(1)} %get-tuple-element.421) | copy-start | bytes 3161092 | tf_op jit(solution)/shard_map/while
  294.8 9.3 %copy-start.13 = (bf16[4,4,343,96]{2,3,1,0:T(8,128)(2,1)}, bf16[4,4,343,96]{2,3,1,0:T(8,128)(2,1)S(1)}, u32[]{:S(2)}) copy-start(bf16[4,4,343,96]{2,3,1,0:T(8,128)(2,1)S(1)} %get-tuple-element.426) | copy-start | bytes 3161092 | tf_op jit(solution)/shard_map/while
  304.3 6.9 %slice-start = ((s8[6340608]{0:T(1024)(128)(4,1)}), s8[4194304]{0:T(1024)(128)(4,1)S(1)}, s32[]{:S(2)}) async-start(s8[6340608]{0:T(1024)(128)(4,1)} %bitcast.279), calls=%async_computation.2 | async-start | bytes 8388608 | tf_op jit(solution)/shard_map/while
  304.3 6.9 %slice-start.1 = ((s8[6340608]{0:T(1024)(128)(4,1)}), s8[2146304]{0:T(1024)(128)(4,1)S(1)}, s32[]{:S(2)}) async-start(s8[6340608]{0:T(1024)(128)(4,1)} %bitcast.279), calls=%async_computation.3 | async-start | bytes 4292608 | tf_op jit(solution)/shard_map/while
  324.7 3.6 copy-start.14
  324.7 3.8 copy-start.10
  328.5 9.3 %copy-start.9 = (bf16[4,4,343,96]{2,3,1,0:T(8,128)(2,1)}, bf16[4,4,343,96]{2,3,1,0:T(8,128)(2,1)S(1)}, u32[]{:S(2)}) copy-start(bf16[4,4,343,96]{2,3,1,0:T(8,128)(2,1)S(1)} %get-tuple-element.421) | copy-start | bytes 3161092 | tf_op jit(solution)/shard_map/while
  328.5 9.3 %copy-start.13 = (bf16[4,4,343,96]{2,3,1,0:T(8,128)(2,1)}, bf16[4,4,343,96]{2,3,1,0:T(8,128)(2,1)S(1)}, u32[]{:S(2)}) copy-start(bf16[4,4,343,96]{2,3,1,0:T(8,128)(2,1)S(1)} %get-tuple-element.426) | copy-start | bytes 3161092 | tf_op jit(solution)/shard_map/while
  338.1 6.9 %slice-start = ((s8[6340608]{0:T(1024)(128)(4,1)}), s8[4194304]{0:T(1024)(128)(4,1)S(1)}, s32[]{:S(2)}) async-start(s8[6340608]{0:T(1024)(128)(4,1)} %bitcast.279), calls=%async_computation.2 | async-start | bytes 8388608 | tf_op jit(solution)/shard_map/while
  338.1 6.9 %slice-start.1 = ((s8[6340608]{0:T(1024)(128)(4,1)}), s8[2146304]{0:T(1024)(128)(4,1)S(1)}, s32[]{:S(2)}) async-start(s8[6340608]{0:T(1024)(128)(4,1)} %bitcast.279), calls=%async_computation.3 | async-start | bytes 4292608 | tf_op jit(solution)/shard_map/while
  358.4 3.6 copy-start.14
  358.5 3.8 copy-start.10
  366.9 81.6 %collective-permute-start.3 = (f32[3,28,7,96]{3,2,1,0:T(8,128)}, f32[3,28,7,96]{3,2,1,0:T(8,128)S(1)}, u32[]{:S(2)}, u32[]{:S(2)}) collective-permute-start(f32[3,28,7,96]{3,2,1,0:T(8,128)} %slice.79), channel_id=1, source_target_pairs={{24,0},{0,8},{8,16},{16,24},{25,1},{1,9},{9,17},{17,25},{26,2},{2,... | collective-permute-start | bytes 677384 | tf_op jit(solution)/shard_map/ppermute | solution.py:13
  388.7 59.7 %copy-start.4 = (f32[25,28,7,96]{3,2,1,0:T(8,128)S(1)}, f32[25,28,7,96]{3,2,1,0:T(8,128)}, u32[]{:S(2)}) copy-start(f32[25,28,7,96]{3,2,1,0:T(8,128)} %slice.80) | copy-start | bytes 5644804
  449.2 38.8 %collective-permute-start.4 = (f32[28,3,7,96]{3,2,1,0:T(8,128)}, f32[28,3,7,96]{3,2,1,0:T(8,128)}, u32[]{:S(2)}, u32[]{:S(2)}) collective-permute-start(f32[28,3,7,96]{3,2,1,0:T(8,128)} %pad_maximum_fusion.4), channel_id=1, source_target_pairs={{6,0},{0,2},{2,4},{4,6},{7,1},{1,3},{3,5},{5,7},{14,8},{8,10},{10,... | collective-permute-start | bytes 677384 | tf_op jit(solution)/shard_map/ppermute | solution.py:13
  487.8 90.3 %all-reduce.7.cloned.1.call-start = ((), (), s32[]{:S(2)}) async-start(), calls=%async_computation.1 | async-start | bytes 294912 | tf_op jit(solution)/shard_map/psum | solution.py:199
  488.0 5.5 copy-start.3
  493.1 90.6 %collective-permute-start.5 = (f32[28,28,3,96]{3,1,2,0:T(8,128)}, f32[28,28,3,96]{3,1,2,0:T(8,128)S(1)}, u32[]{:S(2)}, u32[]{:S(2)}) collective-permute-start(f32[28,28,3,96]{3,1,2,0:T(8,128)} %copy.86), channel_id=1, source_target_pairs={{1,0},{0,1},{3,2},{2,3},{5,4},{4,5},{7,6},{6,7},{9,8},{8,9},{11,10... | collective-permute-start | bytes 2709512 | tf_op jit(solution)/shard_map/ppermute | solution.py:13
  579.7 5.3 copy-start.2
  579.7 5.3 copy-start.26
  585.0 6.4 copy-start.8
  585.4 55.7 %copy-start.6 = (bf16[28,28,7,96]{3,2,1,0:T(8,128)(2,1)S(1)}, bf16[28,28,7,96]{3,2,1,0:T(8,128)(2,1)}, u32[]{:S(2)}) copy-start(bf16[28,28,7,96]{3,2,1,0:T(8,128)(2,1)} %param.11) | copy-start | bytes 3161092
  (8 other events, 18.0 us)
Sparse Core Ops, SparseCore 0:
  487.9 52.5 all-reduce.4
  542.8 35.2 all-reduce.6
